TPU v7x, 32 devices: a whole 2x2x4 slice. The times are simulated.
32 devices in a mesh: dp: 8 (over y, x, core), mp: 4 (over z).
Axes of the slice: x: 2, y: 2, z: 4, core: 2. Of those that a mesh axis runs over, the one named last changes fastest.
Arguments:
- images: bfloat16 [1536, 1024], P('dp', 'mp'), may hold values from -80 to 80, as said below
- texts: bfloat16 [1536, 1024], P('dp', 'mp'), may hold values from -80 to 80, as said below
- logit_scale: float32 [1], replicated, may hold values from 240 to 300
Outputs:
- row_loss: float32 [1536], P('dp')
- column_loss: float32 [1536], P('dp')
Inputs may be any that keep to these rules, and one draw needn't show every extreme that they name: `images`: Real-valued entries. `texts`: Real-valued entries.
All inputs are finite; a program needn't handle non-finite values.
Results may differ from a plain program's by a relative error of at most 0.0044.
Values may be sent and summed in bfloat16 or wider, within the bound.
No kernel may reach another device: no remote copies, remote signals or barrier semaphores. Data moves between devices by JAX's collectives and lax.ppermute only.
A program may use at most 64 MiB of HBM per device.

v0:
```python
import functools

import jax
import jax.numpy as jnp
from jax import lax
from jax.experimental import pallas as pl
from jax.experimental.pallas import tpu as pltpu
from jax.sharding import PartitionSpec as P


AXES = ("dp", "mp")
LANES = 128
F32 = jnp.float32
BF16 = jnp.bfloat16


def normalize(rows):
    values = rows.astype(F32)
    return (values * lax.rsqrt(jnp.sum(values * values, axis=1, keepdims=True) + 1e-06)).astype(
        BF16
    )


def shift(x, axis, step):
    return lax.ppermute(x, axis, [(i, i ^ step) for i in range(lax.axis_size(axis))])


def local_kernel(body, out_shape, operands, out_memory=pltpu.VMEM):
    outs = jax.tree.leaves(out_shape)
    return pl.pallas_call(
        body,
        out_shape=out_shape,
        in_specs=[pl.BlockSpec(memory_space=pltpu.VMEM)] * len(operands),
        out_specs=jax.tree.map(lambda _: pl.BlockSpec(memory_space=out_memory), out_shape),
        compiler_params=pltpu.CompilerParams(vmem_limit_bytes=8 * 2**20),
    )(*operands)


def split_body(quarter, texts_ref, *refs):
    half = len(refs) // 2
    k = lax.axis_index("mp")
    copies = []
    for s, (out_ref, sem) in enumerate(zip(refs[:half], refs[half:])):
        start = pl.multiple_of((k ^ s) * quarter, 8)
        copies.append(pltpu.make_async_copy(texts_ref.at[pl.ds(start, quarter)], out_ref, sem))
    for copy in copies:
        copy.start()
    for copy in copies:
        copy.wait()


def unit_body(*refs):
    out_ref = refs[-1]
    parts = [ref[...].astype(F32) for ref in refs[:-1]]
    total = sum(jnp.sum(part * part, axis=1, keepdims=True) for part in parts)
    inverse = lax.rsqrt(total + 1e-06)
    width = parts[0].shape[1]
    for s, part in enumerate(parts):
        out_ref[:, s * width : (s + 1) * width] = (part * inverse).astype(BF16)


def to_lanes(column):
    shape = (column.shape[0], LANES)
    row = lax.broadcasted_iota(jnp.int32, shape, 0)
    lane = lax.broadcasted_iota(jnp.int32, shape, 1)
    return jnp.sum(jnp.where(row == lane, column, 0.0), axis=0, keepdims=True)


def stats_body(n, q, scale_ref, *refs):
    image_refs, text_refs, out_ref = refs[:2], refs[2:-1], refs[-1]
    i = lax.axis_index("dp")
    k = lax.axis_index("mp")
    rows = image_refs[0].shape[0]
    quarter = text_refs[0].shape[0]
    text = jnp.concatenate([ref[...] for ref in text_refs], axis=0)
    scores = [
        scale_ref[0]
        * lax.dot_general(
            text, ref[...], (((1,), (1,)), ((), ())), preferred_element_type=F32
        )
        for ref in image_refs
    ]
    row_lse = []
    for part in scores:
        top = jnp.max(part, axis=0, keepdims=True)
        row_lse.append(top + jnp.log(jnp.sum(jnp.exp(part - top), axis=0, keepdims=True)))
    top = jnp.max(jnp.maximum(*scores), axis=1, keepdims=True)
    total = jnp.exp(scores[0] - top) + jnp.exp(scores[1] - top)
    col_lse = top + jnp.log(jnp.sum(total, axis=1, keepdims=True))
    own = scores[0][:quarter]
    row = lax.broadcasted_iota(jnp.int32, own.shape, 0)
    lane = lax.broadcasted_iota(jnp.int32, own.shape, 1)
    matched = jnp.sum(jnp.where(row + k * quarter == lane, own, 0.0), axis=1, keepdims=True)
    matched = to_lanes(matched)
    spare = jnp.zeros((1, 2 * LANES - rows), F32)
    wide = [jnp.concatenate([lse, spare], axis=1) for lse in row_lse]
    for d in range(n):
        lse = wide[d % 2]
        col = to_lanes(col_lse[d // 2 * quarter : (d // 2 + 1) * quarter])
        block = jnp.concatenate([lse[:, :LANES], lse[:, LANES:], col, matched], axis=0)
        for m in range(q):
            out_ref[(i ^ d) * q + m] = block


def finish_body(n, q, rows, got_ref, row_ref, col_ref):
    i = lax.axis_index("dp")
    quarter = rows // q

    def merge(parts):
        peak = functools.reduce(jnp.maximum, parts)
        return peak + jnp.log(sum(jnp.exp(x - peak) for x in parts))

    lse = merge([got_ref[(i ^ d) * q + m] for d in range(2) for m in range(q)])
    row_lse = jnp.concatenate([lse[0:1], lse[1:2]], axis=1)[:, :rows]
    own = [got_ref[i * q + m] for m in range(q)]
    matched = jnp.concatenate([x[3:4, :quarter] for x in own], axis=1)
    cols = []
    for m in range(q):
        lse = merge([got_ref[(i ^ d) * q + m] for d in range(0, n, 2)])
        cols.append(lse[2:3, :quarter])
    row_ref[...] = (row_lse - matched).reshape(rows)
    col_ref[...] = (jnp.concatenate(cols, axis=1) - matched).reshape(rows)


def cube(images, texts, logit_scale):
    n = lax.axis_size("dp")
    q = lax.axis_size("mp")
    rows, width = images.shape
    quarter = rows // q
    part = jax.ShapeDtypeStruct((quarter, width), BF16)
    text_parts = pl.pallas_call(
        functools.partial(split_body, quarter),
        out_shape=[part] * q,
        in_specs=[pl.BlockSpec(memory_space=pl.ANY)],
        out_specs=[pl.BlockSpec(memory_space=pltpu.VMEM)] * q,
        scratch_shapes=[pltpu.SemaphoreType.DMA] * q,
        compiler_params=pltpu.CompilerParams(vmem_limit_bytes=8 * 2**20),
    )(pltpu.with_memory_space_constraint(texts, pltpu.HBM))
    got = [text_parts[0]]
    for s in range(1, q):
        got.append(shift(text_parts[s], "mp", s))
    image_parts = [images]
    for s in range(1, q):
        image_parts.append(shift(images, "mp", s))
    other_parts = []
    for s in range(q):
        other_parts.append(shift(image_parts[s], "dp", 1))
    text_unit = local_kernel(unit_body, jax.ShapeDtypeStruct((quarter, q * width), BF16), got)
    blocks = [text_unit]
    for d in range(2, n, 2):
        blocks.append(shift(text_unit, "dp", d))
    full = jax.ShapeDtypeStruct((rows, q * width), BF16)
    image_unit = local_kernel(unit_body, full, image_parts)
    other_unit = local_kernel(unit_body, full, other_parts)
    operands = [image_unit, other_unit, *blocks]
    message = pl.pallas_call(
        functools.partial(stats_body, n, q),
        out_shape=jax.ShapeDtypeStruct((n * q, 4, LANES), F32),
        in_specs=[pl.BlockSpec(memory_space=pltpu.SMEM)]
        + [pl.BlockSpec(memory_space=pltpu.VMEM)] * len(operands),
        out_specs=pl.BlockSpec(memory_space=pltpu.VMEM),
        compiler_params=pltpu.CompilerParams(vmem_limit_bytes=8 * 2**20),
    )(logit_scale, *operands)
    answer = lax.all_to_all(message, AXES, 0, 0, tiled=True)
    loss = jax.ShapeDtypeStruct((rows,), F32)
    row_loss, column_loss = local_kernel(
        functools.partial(finish_body, n, q, rows), [loss, loss], [answer]
    )
    return row_loss, column_loss


def gathered(images, texts, logit_scale):
    n = lax.axis_size("dp")
    q = lax.axis_size("mp")
    i = lax.axis_index("dp")
    k = lax.axis_index("mp")
    scale = logit_scale[0]
    rows = images.shape[0]
    quarter = rows // q
    image_unit = normalize(lax.all_gather(images, "mp", axis=1, tiled=True))
    text_unit = normalize(lax.all_to_all(texts, "mp", split_axis=0, concat_axis=1, tiled=True))
    all_texts = lax.all_gather(text_unit, "dp", axis=0, tiled=True)
    scores = scale * lax.dot_general(
        image_unit, all_texts, (((1,), (1,)), ((), ())), preferred_element_type=F32
    )
    row_top = jnp.max(scores, axis=1)
    row_lse = row_top + jnp.log(jnp.sum(jnp.exp(scores - row_top[:, None]), axis=1))
    col_top = jnp.max(scores, axis=0)
    col_lse = col_top + jnp.log(jnp.sum(jnp.exp(scores - col_top[None, :]), axis=0))
    mine = lax.dynamic_slice_in_dim(image_unit, k * quarter, quarter, 0)
    matched = scale * jnp.sum(mine.astype(F32) * text_unit.astype(F32), axis=1)
    pieces = [
        jnp.broadcast_to(row_lse[None], (n, rows)),
        jnp.broadcast_to(matched[None], (n, quarter)),
        col_lse.reshape(n, quarter),
    ]
    message = jnp.concatenate(pieces, axis=1)
    size = message.shape[1]
    lanes = -(-size // LANES) * LANES
    message = jnp.pad(message, ((0, 0), (0, lanes - size)))
    message = jnp.broadcast_to(message[:, None, :], (n, q, lanes)).reshape(n * q, -1, LANES)
    got = lax.all_to_all(message, AXES, 0, 0, tiled=True).reshape(n, q, lanes)
    own = lax.dynamic_index_in_dim(got, i, 0, False)
    row_parts = own[:, :rows]
    peak = jnp.max(row_parts, axis=0)
    row_out = peak + jnp.log(jnp.sum(jnp.exp(row_parts - peak), axis=0))
    matched = own[:, rows : rows + quarter].reshape(rows)
    col_parts = got[:, :, rows + quarter : size]
    peak = jnp.max(col_parts, axis=0)
    col_out = (peak + jnp.log(jnp.sum(jnp.exp(col_parts - peak), axis=0))).reshape(rows)
    return row_out - matched, col_out - matched


def on_device(images, texts, logit_scale):
    n = lax.axis_size("dp")
    q = lax.axis_size("mp")
    power = n & (n - 1) == 0 and q & (q - 1) == 0
    rows, width = images.shape
    fits = LANES < rows <= 2 * LANES and rows // q <= LANES and width % LANES == 0
    if power and n <= 8 and q <= 4 and fits and (rows // q) % 16 == 0:
        return cube(images, texts, logit_scale)
    return gathered(images, texts, logit_scale)


def solution(mesh):
    return jax.shard_map(
        on_device,
        mesh=mesh,
        in_specs=(P("dp", "mp"), P("dp", "mp"), P()),
        out_specs=(P("dp"), P("dp")),
        check_vma=False,
    )
```

profile of v0, /device:TPU:0, one launch (start us, length us, event | category | flops | bytes accessed | tf_op | source)
XLA Modules:
  0.0 46.0 jit_solution(6244860819558666669)
XLA Ops:
  0.6 3.1 %collective-permute-start = (bf16[192,256]{1,0:T(8,128)(2,1)}, bf16[192,256]{1,0:T(8,128)(2,1)S(1)}, u32[]{:S(2)}, u32[]{:S(2)}) collective-permute-start(bf16[192,256]{1,0:T(8,128)(2,1)} %refs_0_.1), channel_id=1, source_target_pairs={{0,1},{1,0},{2,3},{3,2},{4,5},{5,4},{6,7},{7,6},{8,9},{9,8},{10,11... | collective-permute-start | bytes 294920 | tf_op jit(solution)/shard_map/ppermute | solution.py:25
  3.7 2.6 %collective-permute-start.1 = (bf16[192,256]{1,0:T(8,128)(2,1)}, bf16[192,256]{1,0:T(8,128)(2,1)S(1)}, u32[]{:S(2)}, u32[]{:S(2)}) collective-permute-start(bf16[192,256]{1,0:T(8,128)(2,1)} %refs_0_.1), channel_id=1, source_target_pairs={{0,2},{1,3},{2,0},{3,1},{4,6},{5,7},{6,4},{7,5},{8,10},{9,11},{10,... | collective-permute-start | bytes 294920 | tf_op jit(solution)/shard_map/ppermute | solution.py:25
  6.3 0.0 collective-permute-start.2
  6.3 0.4 collective-permute-done.refs_1_
  6.8 0.1 collective-permute-start.4
  6.9 0.8 %shard_map.52 = (bf16[48,256]{1,0:T(8,128)(2,1)S(1)}, bf16[48,256]{1,0:T(8,128)(2,1)S(1)}, bf16[48,256]{1,0:T(8,128)(2,1)S(1)}, bf16[48,256]{1,0:T(8,128)(2,1)S(1)}) custom-call(bf16[192,256]{1,0:T(8,128)(2,1)} %texts_ref.1), custom_call_target="tpu_custom_call" | custom-call | tf_op jit(solution)/shard_map/pallas_call | solution.py:131
  7.7 1.8 %collective-permute-start.7 = (bf16[48,256]{1,0:T(8,128)(2,1)S(1)}, bf16[48,256]{1,0:T(8,128)(2,1)S(1)}, u32[]{:S(2)}, u32[]{:S(2)}) collective-permute-start(bf16[48,256]{1,0:T(8,128)(2,1)S(1)} %get-tuple-element.7), channel_id=1, source_target_pairs={{0,1},{1,0},{2,3},{3,2},{4,5},{5,4},{6,7},{7,6},{8,9},{9,8},{10,11... | collective-permute-start | bytes 73736 | tf_op jit(solution)/shard_map/ppermute | solution.py:25
  9.5 2.4 %collective-permute-done.7.refs_1_ = bf16[48,256]{1,0:T(8,128)(2,1)S(1)} collective-permute-done((bf16[48,256]{1,0:T(8,128)(2,1)S(1)}, bf16[48,256]{1,0:T(8,128)(2,1)S(1)}, u32[]{:S(2)}, u32[]{:S(2)}) %collective-permute-start.7) | collective-permute-done | bytes 24608 | tf_op jit(solution)/shard_map/ppermute | solution.py:25
  11.9 3.4 %collective-permute-start.8 = (bf16[48,256]{1,0:T(8,128)(2,1)S(1)}, bf16[48,256]{1,0:T(8,128)(2,1)S(1)}, u32[]{:S(2)}, u32[]{:S(2)}) collective-permute-start(bf16[48,256]{1,0:T(8,128)(2,1)S(1)} %get-tuple-element.8), channel_id=1, source_target_pairs={{0,2},{1,3},{2,0},{3,1},{4,6},{5,7},{6,4},{7,5},{8,10},{9,11},{10,... | collective-permute-start | bytes 73736 | tf_op jit(solution)/shard_map/ppermute | solution.py:25
  15.3 1.8 %collective-permute-done.8.refs_2_ = bf16[48,256]{1,0:T(8,128)(2,1)S(1)} collective-permute-done((bf16[48,256]{1,0:T(8,128)(2,1)S(1)}, bf16[48,256]{1,0:T(8,128)(2,1)S(1)}, u32[]{:S(2)}, u32[]{:S(2)}) %collective-permute-start.8) | collective-permute-done | bytes 24608 | tf_op jit(solution)/shard_map/ppermute | solution.py:25
  17.1 4.3 %collective-permute-start.9 = (bf16[48,256]{1,0:T(8,128)(2,1)S(1)}, bf16[48,256]{1,0:T(8,128)(2,1)S(1)}, u32[]{:S(2)}, u32[]{:S(2)}) collective-permute-start(bf16[48,256]{1,0:T(8,128)(2,1)S(1)} %get-tuple-element.9), channel_id=1, source_target_pairs={{0,3},{1,2},{2,1},{3,0},{4,7},{5,6},{6,5},{7,4},{8,11},{9,10},{10,... | collective-permute-start | bytes 73736 | tf_op jit(solution)/shard_map/ppermute | solution.py:25
  21.4 1.8 %collective-permute-done.9.refs_3_ = bf16[48,256]{1,0:T(8,128)(2,1)S(1)} collective-permute-done((bf16[48,256]{1,0:T(8,128)(2,1)S(1)}, bf16[48,256]{1,0:T(8,128)(2,1)S(1)}, u32[]{:S(2)}, u32[]{:S(2)}) %collective-permute-start.9) | collective-permute-done | bytes 24608 | tf_op jit(solution)/shard_map/ppermute | solution.py:25
  23.2 0.1 shard_map.53.refs_2_
  23.3 1.6 %collective-permute-start.10 = (bf16[48,1024]{1,0:T(8,128)(2,1)S(1)}, bf16[48,1024]{1,0:T(8,128)(2,1)S(1)}, u32[]{:S(2)}, u32[]{:S(2)}) collective-permute-start(bf16[48,1024]{1,0:T(8,128)(2,1)S(1)} %shard_map.53.refs_2_), channel_id=1, source_target_pairs={{0,8},{4,12},{8,0},{12,4},{16,24},{20,28},{24,16},{28,20},{1,9},{5... | collective-permute-start | bytes 294920 | tf_op jit(solution)/shard_map/ppermute | solution.py:25
  24.9 0.5 %collective-permute-start.6 = (bf16[192,256]{1,0:T(8,128)(2,1)S(1)}, bf16[192,256]{1,0:T(8,128)(2,1)S(1)}, u32[]{:S(2)}, u32[]{:S(2)}) collective-permute-start(bf16[192,256]{1,0:T(8,128)(2,1)S(1)} %collective-permute-done.2.refs_3_), channel_id=1, source_target_pairs={{0,4},{4,0},{8,12},{12,8},{16,20},{20,16},{24,28},{28,24},{1,5},{5... | collective-permute-start | bytes 294920 | tf_op jit(solution)/shard_map/ppermute | solution.py:25
  25.4 1.5 %collective-permute-start.11 = (bf16[48,1024]{1,0:T(8,128)(2,1)S(1)}, bf16[48,1024]{1,0:T(8,128)(2,1)S(1)}, u32[]{:S(2)}, u32[]{:S(2)}) collective-permute-start(bf16[48,1024]{1,0:T(8,128)(2,1)S(1)} %shard_map.53.refs_2_), channel_id=1, source_target_pairs={{0,16},{4,20},{8,24},{12,28},{16,0},{20,4},{24,8},{28,12},{1,17},{... | collective-permute-start | bytes 294920 | tf_op jit(solution)/shard_map/ppermute | solution.py:25
  26.9 0.5 %collective-permute-start.12 = (bf16[48,1024]{1,0:T(8,128)(2,1)S(1)}, bf16[48,1024]{1,0:T(8,128)(2,1)S(1)}, u32[]{:S(2)}, u32[]{:S(2)}) collective-permute-start(bf16[48,1024]{1,0:T(8,128)(2,1)S(1)} %shard_map.53.refs_2_), channel_id=1, source_target_pairs={{0,24},{4,28},{8,16},{12,20},{16,8},{20,12},{24,0},{28,4},{1,25},{... | collective-permute-start | bytes 294920 | tf_op jit(solution)/shard_map/ppermute | solution.py:25
  28.0 0.2 shard_map.50.refs_0_
  28.3 0.2 shard_map.51.refs_1_
  28.5 2.8 %collective-permute-done.11.refs_4_ = bf16[48,1024]{1,0:T(8,128)(2,1)S(1)} collective-permute-done((bf16[48,1024]{1,0:T(8,128)(2,1)S(1)}, bf16[48,1024]{1,0:T(8,128)(2,1)S(1)}, u32[]{:S(2)}, u32[]{:S(2)}) %collective-permute-start.11) | collective-permute-done | bytes 98336 | tf_op jit(solution)/shard_map/ppermute | solution.py:25
  31.3 1.1 %collective-permute-done.12.refs_5_ = bf16[48,1024]{1,0:T(8,128)(2,1)S(1)} collective-permute-done((bf16[48,1024]{1,0:T(8,128)(2,1)S(1)}, bf16[48,1024]{1,0:T(8,128)(2,1)S(1)}, u32[]{:S(2)}, u32[]{:S(2)}) %collective-permute-start.12) | collective-permute-done | bytes 98336 | tf_op jit(solution)/shard_map/ppermute | solution.py:25
  32.4 0.6 %shard_map.54 = f32[32,4,128]{2,1,0:T(4,128)S(1)} custom-call(f32[1]{0:T(128)S(6)} %copy.5.scale_ref, bf16[192,1024]{1,0:T(8,128)(2,1)S(1)} %shard_map.50.refs_0_, bf16[192,1024]{1,0:T(8,128)(2,1)S(1)} %shard_map.51.refs_1_, bf16[48,1024]{1,0:T(8,128)(2,1)S(1)} %shard_map.53.refs_2_, bf16[48,1024]{1,0:T(8,128)(2,1)S(1)} %collective-permute-done.10.refs_3_, ...), custom_call_target="tpu_custom_call" | custom-call | tf_op jit(solution)/shard_map/pallas_call | solution.py:156
  33.0 12.3 %all_to_all.5.got_ref = f32[32,4,128]{2,1,0:T(4,128)S(1)} all-to-all(f32[32,4,128]{2,1,0:T(4,128)S(1)} %shard_map.54), channel_id=1, replica_groups=mesh['dp'=8,'mp'=4] {'dp','mp'}, dimensions={0} | all-to-all | bytes 131072 | tf_op jit(solution)/shard_map/all_to_all | solution.py:164
  45.3 0.7 %shard_map.55 = (f32[192]{0:T(256)}, f32[192]{0:T(256)}) custom-call(f32[32,4,128]{2,1,0:T(4,128)S(1)} %all_to_all.5.got_ref), custom_call_target="tpu_custom_call" | custom-call | tf_op jit(solution)/shard_map/pallas_call | solution.py:30
  (11 shorter events, 0.0 us)
Async XLA Ops:
  0.6 6.1 %collective-permute-start = (bf16[192,256]{1,0:T(8,128)(2,1)}, bf16[192,256]{1,0:T(8,128)(2,1)S(1)}, u32[]{:S(2)}, u32[]{:S(2)}) collective-permute-start(bf16[192,256]{1,0:T(8,128)(2,1)} %refs_0_.1), channel_id=1, source_target_pairs={{0,1},{1,0},{2,3},{3,2},{4,5},{5,4},{6,7},{7,6},{8,9},{9,8},{10,11... | collective-permute-start | bytes 294920 | tf_op jit(solution)/shard_map/ppermute | solution.py:25
  3.7 21.1 %collective-permute-start.1 = (bf16[192,256]{1,0:T(8,128)(2,1)}, bf16[192,256]{1,0:T(8,128)(2,1)S(1)}, u32[]{:S(2)}, u32[]{:S(2)}) collective-permute-start(bf16[192,256]{1,0:T(8,128)(2,1)} %refs_0_.1), channel_id=1, source_target_pairs={{0,2},{1,3},{2,0},{3,1},{4,6},{5,7},{6,4},{7,5},{8,10},{9,11},{10,... | collective-permute-start | bytes 294920 | tf_op jit(solution)/shard_map/ppermute | solution.py:25
  6.3 18.5 %collective-permute-start.2 = (bf16[192,256]{1,0:T(8,128)(2,1)}, bf16[192,256]{1,0:T(8,128)(2,1)S(1)}, u32[]{:S(2)}, u32[]{:S(2)}) collective-permute-start(bf16[192,256]{1,0:T(8,128)(2,1)} %refs_0_.1), channel_id=1, source_target_pairs={{0,3},{1,2},{2,1},{3,0},{4,7},{5,6},{6,5},{7,4},{8,11},{9,10},{10,... | collective-permute-start | bytes 294920 | tf_op jit(solution)/shard_map/ppermute | solution.py:25
  6.3 19.0 %collective-permute-start.3 = (bf16[192,256]{1,0:T(8,128)(2,1)}, bf16[192,256]{1,0:T(8,128)(2,1)S(1)}, u32[]{:S(2)}, u32[]{:S(2)}) collective-permute-start(bf16[192,256]{1,0:T(8,128)(2,1)} %refs_0_.1), channel_id=1, source_target_pairs={{0,4},{4,0},{8,12},{12,8},{16,20},{20,16},{24,28},{28,24},{1,5},{5... | collective-permute-start | bytes 294920 | tf_op jit(solution)/shard_map/ppermute | solution.py:25
  6.8 20.1 %collective-permute-start.4 = (bf16[192,256]{1,0:T(8,128)(2,1)S(1)}, bf16[192,256]{1,0:T(8,128)(2,1)S(1)}, u32[]{:S(2)}, u32[]{:S(2)}) collective-permute-start(bf16[192,256]{1,0:T(8,128)(2,1)S(1)} %collective-permute-done.refs_1_), channel_id=1, source_target_pairs={{0,4},{4,0},{8,12},{12,8},{16,20},{20,16},{24,28},{28,24},{1,5},{5... | collective-permute-start | bytes 294920 | tf_op jit(solution)/shard_map/ppermute | solution.py:25
  7.7 4.2 %collective-permute-start.7 = (bf16[48,256]{1,0:T(8,128)(2,1)S(1)}, bf16[48,256]{1,0:T(8,128)(2,1)S(1)}, u32[]{:S(2)}, u32[]{:S(2)}) collective-permute-start(bf16[48,256]{1,0:T(8,128)(2,1)S(1)} %get-tuple-element.7), channel_id=1, source_target_pairs={{0,1},{1,0},{2,3},{3,2},{4,5},{5,4},{6,7},{7,6},{8,9},{9,8},{10,11... | collective-permute-start | bytes 73736 | tf_op jit(solution)/shard_map/ppermute | solution.py:25
  11.9 5.2 %collective-permute-start.8 = (bf16[48,256]{1,0:T(8,128)(2,1)S(1)}, bf16[48,256]{1,0:T(8,128)(2,1)S(1)}, u32[]{:S(2)}, u32[]{:S(2)}) collective-permute-start(bf16[48,256]{1,0:T(8,128)(2,1)S(1)} %get-tuple-element.8), channel_id=1, source_target_pairs={{0,2},{1,3},{2,0},{3,1},{4,6},{5,7},{6,4},{7,5},{8,10},{9,11},{10,... | collective-permute-start | bytes 73736 | tf_op jit(solution)/shard_map/ppermute | solution.py:25
  17.1 6.1 %collective-permute-start.9 = (bf16[48,256]{1,0:T(8,128)(2,1)S(1)}, bf16[48,256]{1,0:T(8,128)(2,1)S(1)}, u32[]{:S(2)}, u32[]{:S(2)}) collective-permute-start(bf16[48,256]{1,0:T(8,128)(2,1)S(1)} %get-tuple-element.9), channel_id=1, source_target_pairs={{0,3},{1,2},{2,1},{3,0},{4,7},{5,6},{6,5},{7,4},{8,11},{9,10},{10,... | collective-permute-start | bytes 73736 | tf_op jit(solution)/shard_map/ppermute | solution.py:25
  23.2 4.9 %copy-start = (bf16[192,256]{1,0:T(8,128)(2,1)S(1)}, bf16[192,256]{1,0:T(8,128)(2,1)}, u32[]{:S(2)}) copy-start(bf16[192,256]{1,0:T(8,128)(2,1)} %refs_0_.1) | copy-start | bytes 294916
  23.3 5.2 %collective-permute-start.10 = (bf16[48,1024]{1,0:T(8,128)(2,1)S(1)}, bf16[48,1024]{1,0:T(8,128)(2,1)S(1)}, u32[]{:S(2)}, u32[]{:S(2)}) collective-permute-start(bf16[48,1024]{1,0:T(8,128)(2,1)S(1)} %shard_map.53.refs_2_), channel_id=1, source_target_pairs={{0,8},{4,12},{8,0},{12,4},{16,24},{20,28},{24,16},{28,20},{1,9},{5... | collective-permute-start | bytes 294920 | tf_op jit(solution)/shard_map/ppermute | solution.py:25
  24.9 3.4 %collective-permute-start.5 = (bf16[192,256]{1,0:T(8,128)(2,1)S(1)}, bf16[192,256]{1,0:T(8,128)(2,1)S(1)}, u32[]{:S(2)}, u32[]{:S(2)}) collective-permute-start(bf16[192,256]{1,0:T(8,128)(2,1)S(1)} %collective-permute-done.1.refs_2_), channel_id=1, source_target_pairs={{0,4},{4,0},{8,12},{12,8},{16,20},{20,16},{24,28},{28,24},{1,5},{5... | collective-permute-start | bytes 294920 | tf_op jit(solution)/shard_map/ppermute | solution.py:25
  24.9 3.4 %collective-permute-start.6 = (bf16[192,256]{1,0:T(8,128)(2,1)S(1)}, bf16[192,256]{1,0:T(8,128)(2,1)S(1)}, u32[]{:S(2)}, u32[]{:S(2)}) collective-permute-start(bf16[192,256]{1,0:T(8,128)(2,1)S(1)} %collective-permute-done.2.refs_3_), channel_id=1, source_target_pairs={{0,4},{4,0},{8,12},{12,8},{16,20},{20,16},{24,28},{28,24},{1,5},{5... | collective-permute-start | bytes 294920 | tf_op jit(solution)/shard_map/ppermute | solution.py:25
  25.4 5.9 %collective-permute-start.11 = (bf16[48,1024]{1,0:T(8,128)(2,1)S(1)}, bf16[48,1024]{1,0:T(8,128)(2,1)S(1)}, u32[]{:S(2)}, u32[]{:S(2)}) collective-permute-start(bf16[48,1024]{1,0:T(8,128)(2,1)S(1)} %shard_map.53.refs_2_), channel_id=1, source_target_pairs={{0,16},{4,20},{8,24},{12,28},{16,0},{20,4},{24,8},{28,12},{1,17},{... | collective-permute-start | bytes 294920 | tf_op jit(solution)/shard_map/ppermute | solution.py:25
  26.9 5.5 %collective-permute-start.12 = (bf16[48,1024]{1,0:T(8,128)(2,1)S(1)}, bf16[48,1024]{1,0:T(8,128)(2,1)S(1)}, u32[]{:S(2)}, u32[]{:S(2)}) collective-permute-start(bf16[48,1024]{1,0:T(8,128)(2,1)S(1)} %shard_map.53.refs_2_), channel_id=1, source_target_pairs={{0,24},{4,28},{8,16},{12,20},{16,8},{20,12},{24,0},{28,4},{1,25},{... | collective-permute-start | bytes 294920 | tf_op jit(solution)/shard_map/ppermute | solution.py:25
where the time goes:
time: 46.2 us; the launch traced here: 46 us
  starting transfers between devices  19.3 us (42%)
  blocking collectives  12.3 us (27%)
  waiting for transfers between devices  10.4 us (23%)
  Pallas kernels  2.6 us (6%)
  between operations  1.37 us (3%)
    ppermute x13, starting transfers between devices, shift(): lax.ppermute(x, axis, [(i, i ^ step) for i in range(lax.axis_size(axis))])  19.3 us
    all_to_all x1, blocking collectives, cube(): answer = lax.all_to_all(message, AXES, 0, 0, tiled=True)  12.3 us
    ppermute x13, waiting for transfers between devices, shift(): lax.ppermute(x, axis, [(i, i ^ step) for i in range(lax.axis_size(axis))])  10.4 us
    pallas_call x4, Pallas kernels, local_kernel(): pl.pallas_call(body, out_shape=out_shape, in_specs=[pl.BlockSpec(memory_s...  1.2 us
  transfers between devices with their start and end apart: 13, of which 6 were waited for; matrix products, arithmetic and copies ran while one was open for 0% of the time, Pallas kernels for 3%

commit v1 on v0

--- a/solution.py
+++ b/solution.py
@@ -12,6 +12,7 @@
 LANES = 128
 F32 = jnp.float32
 BF16 = jnp.bfloat16
+COST = 50_000_000
 
 
 def normalize(rows):
@@ -36,17 +37,11 @@
     )(*operands)
 
 
-def split_body(quarter, texts_ref, *refs):
-    half = len(refs) // 2
+def split_body(quarter, texts_ref, *out_refs):
     k = lax.axis_index("mp")
-    copies = []
-    for s, (out_ref, sem) in enumerate(zip(refs[:half], refs[half:])):
+    for s, out_ref in enumerate(out_refs):
         start = pl.multiple_of((k ^ s) * quarter, 8)
-        copies.append(pltpu.make_async_copy(texts_ref.at[pl.ds(start, quarter)], out_ref, sem))
-    for copy in copies:
-        copy.start()
-    for copy in copies:
-        copy.wait()
+        out_ref[...] = texts_ref[pl.ds(start, quarter), :]
 
 
 def unit_body(*refs):
@@ -59,22 +54,34 @@
         out_ref[:, s * width : (s + 1) * width] = (part * inverse).astype(BF16)
 
 
-def to_lanes(column):
-    shape = (column.shape[0], LANES)
-    row = lax.broadcasted_iota(jnp.int32, shape, 0)
-    lane = lax.broadcasted_iota(jnp.int32, shape, 1)
-    return jnp.sum(jnp.where(row == lane, column, 0.0), axis=0, keepdims=True)
+def fetch_unit_body(images_ref, *refs):
+    part_refs, (own_ref, sem) = refs[:-2], refs[-2:]
+    copy = pltpu.make_async_copy(images_ref, own_ref, sem)
+    copy.start()
+    copy.wait()
+    unit_body(own_ref, *part_refs)
+
+
+def diagonal_body(out_ref):
+    row = lax.broadcasted_iota(jnp.int32, out_ref.shape, 0)
+    lane = lax.broadcasted_iota(jnp.int32, out_ref.shape, 1)
+    out_ref[...] = jnp.where(row == lane, 1.0, 0.0)
+
+
+def to_lanes(column, diagonal):
+    return jnp.sum(jnp.where(diagonal > 0.5, column, 0.0), axis=0, keepdims=True)
 
 
 def stats_body(n, q, scale_ref, *refs):
-    image_refs, text_refs, out_ref = refs[:2], refs[2:-1], refs[-1]
+    diagonal = refs[0][...]
+    image_refs, text_refs, out_ref = refs[1:3], refs[3:-1], refs[-1]
     i = lax.axis_index("dp")
     k = lax.axis_index("mp")
     rows = image_refs[0].shape[0]
     quarter = text_refs[0].shape[0]
     text = jnp.concatenate([ref[...] for ref in text_refs], axis=0)
     scores = [
-        scale_ref[0]
+        scale_ref[...]
         * lax.dot_general(
             text, ref[...], (((1,), (1,)), ((), ())), preferred_element_type=F32
         )
@@ -91,12 +98,12 @@
     row = lax.broadcasted_iota(jnp.int32, own.shape, 0)
     lane = lax.broadcasted_iota(jnp.int32, own.shape, 1)
     matched = jnp.sum(jnp.where(row + k * quarter == lane, own, 0.0), axis=1, keepdims=True)
-    matched = to_lanes(matched)
+    matched = to_lanes(matched, diagonal)
     spare = jnp.zeros((1, 2 * LANES - rows), F32)
     wide = [jnp.concatenate([lse, spare], axis=1) for lse in row_lse]
     for d in range(n):
         lse = wide[d % 2]
-        col = to_lanes(col_lse[d // 2 * quarter : (d // 2 + 1) * quarter])
+        col = to_lanes(col_lse[d // 2 * quarter : (d // 2 + 1) * quarter], diagonal)
         block = jnp.concatenate([lse[:, :LANES], lse[:, LANES:], col, matched], axis=0)
         for m in range(q):
             out_ref[(i ^ d) * q + m] = block
@@ -127,15 +134,15 @@
     q = lax.axis_size("mp")
     rows, width = images.shape
     quarter = rows // q
+    diagonal = pl.pallas_call(
+        diagonal_body,
+        out_shape=jax.ShapeDtypeStruct((quarter, LANES), F32),
+        out_specs=pl.BlockSpec(memory_space=pltpu.VMEM),
+        cost_estimate=pl.CostEstimate(flops=COST, transcendentals=0, bytes_accessed=0),
+        compiler_params=pltpu.CompilerParams(vmem_limit_bytes=8 * 2**20),
+    )()
     part = jax.ShapeDtypeStruct((quarter, width), BF16)
-    text_parts = pl.pallas_call(
-        functools.partial(split_body, quarter),
-        out_shape=[part] * q,
-        in_specs=[pl.BlockSpec(memory_space=pl.ANY)],
-        out_specs=[pl.BlockSpec(memory_space=pltpu.VMEM)] * q,
-        scratch_shapes=[pltpu.SemaphoreType.DMA] * q,
-        compiler_params=pltpu.CompilerParams(vmem_limit_bytes=8 * 2**20),
-    )(pltpu.with_memory_space_constraint(texts, pltpu.HBM))
+    text_parts = local_kernel(functools.partial(split_body, quarter), [part] * q, [texts])
     got = [text_parts[0]]
     for s in range(1, q):
         got.append(shift(text_parts[s], "mp", s))
@@ -150,17 +157,24 @@
     for d in range(2, n, 2):
         blocks.append(shift(text_unit, "dp", d))
     full = jax.ShapeDtypeStruct((rows, q * width), BF16)
-    image_unit = local_kernel(unit_body, full, image_parts)
+    image_unit = pl.pallas_call(
+        fetch_unit_body,
+        out_shape=full,
+        in_specs=[pl.BlockSpec(memory_space=pl.ANY)]
+        + [pl.BlockSpec(memory_space=pltpu.VMEM)] * (q - 1),
+        out_specs=pl.BlockSpec(memory_space=pltpu.VMEM),
+        scratch_shapes=[pltpu.VMEM((rows, width), BF16), pltpu.SemaphoreType.DMA],
+        compiler_params=pltpu.CompilerParams(vmem_limit_bytes=8 * 2**20),
+    )(pltpu.with_memory_space_constraint(images, pltpu.HBM), *image_parts[1:])
     other_unit = local_kernel(unit_body, full, other_parts)
-    operands = [image_unit, other_unit, *blocks]
+    operands = [diagonal, image_unit, other_unit, *blocks]
     message = pl.pallas_call(
         functools.partial(stats_body, n, q),
         out_shape=jax.ShapeDtypeStruct((n * q, 4, LANES), F32),
-        in_specs=[pl.BlockSpec(memory_space=pltpu.SMEM)]
-        + [pl.BlockSpec(memory_space=pltpu.VMEM)] * len(operands),
+        in_specs=[pl.BlockSpec(memory_space=pltpu.VMEM)] * (len(operands) + 1),
         out_specs=pl.BlockSpec(memory_space=pltpu.VMEM),
         compiler_params=pltpu.CompilerParams(vmem_limit_bytes=8 * 2**20),
-    )(logit_scale, *operands)
+    )(logit_scale.reshape(1, 1), *operands)
     answer = lax.all_to_all(message, AXES, 0, 0, tiled=True)
     loss = jax.ShapeDtypeStruct((rows,), F32)
     row_loss, column_loss = local_kernel(

time: 46.2 us -> 46.2 us (level)
  local copies, waits for them, and re-layouts: 0.01 us -> 0.89 us
  waiting for transfers between devices: 10.4 us -> 9.86 us
  blocking collectives: 12.3 us -> 11.8 us
    unnamed x2, local copies, waits for them, and re-layouts: 0.01 us -> 0.89 us
    ppermute x13, waiting for transfers between devices: 10.4 us -> 9.86 us  [shift(): lax.ppermute(x, axis, [(i, i ^ step) for i in range(lax.axis_size(axis))])]
    all_to_all x1, blocking collectives: 12.3 us -> 11.8 us  [cube(): answer = lax.all_to_all(message, AXES, 0, 0, tiled=True)]
    pallas_call x1 -> x2, Pallas kernels: 0.82 us -> 1.12 us  [the longest x1 1.11 us: cube(): pl.pallas_call(fetch_unit_body, out_shape=full, in_specs=[pl.BlockSpec(me...]
where the time goes in v1:
time: 46.2 us; the launch traced here: 46 us
  starting transfers between devices  19.4 us (42%)
  blocking collectives  11.8 us (26%)
  waiting for transfers between devices  9.86 us (21%)
  Pallas kernels  2.7 us (6%)
  between operations  1.36 us (3%)
  local copies, waits for them, and re-layouts  0.89 us (2%)
    ppermute x13, starting transfers between devices, shift(): lax.ppermute(x, axis, [(i, i ^ step) for i in range(lax.axis_size(axis))])  19.4 us
    all_to_all x1, blocking collectives, cube(): answer = lax.all_to_all(message, AXES, 0, 0, tiled=True)  11.8 us
    ppermute x13, waiting for transfers between devices, shift(): lax.ppermute(x, axis, [(i, i ^ step) for i in range(lax.axis_size(axis))])  9.86 us
    pallas_call x1, Pallas kernels, cube(): pl.pallas_call(fetch_unit_body, out_shape=full, in_specs=[pl.BlockSpec(me...  1.11 us
    pallas_call x4, Pallas kernels, local_kernel(): pl.pallas_call(body, out_shape=out_shape, in_specs=[pl.BlockSpec(memory_s...  0.99 us
  transfers between devices with their start and end apart: 13, of which 6 were waited for; matrix products, arithmetic and copies ran while one was open for 0% of the time, Pallas kernels for 3%

profile of v1, /device:TPU:0, one launch (start us, length us, event | category | flops | bytes accessed | tf_op | source)
XLA Modules:
  0.0 46.0 jit_solution(17604263430020021917)
XLA Ops:
  0.6 3.1 %collective-permute-start = (bf16[192,256]{1,0:T(8,128)(2,1)}, bf16[192,256]{1,0:T(8,128)(2,1)S(1)}, u32[]{:S(2)}, u32[]{:S(2)}) collective-permute-start(bf16[192,256]{1,0:T(8,128)(2,1)} %images_ref.1), channel_id=1, source_target_pairs={{0,1},{1,0},{2,3},{3,2},{4,5},{5,4},{6,7},{7,6},{8,9},{9,8},{10,11... | collective-permute-start | bytes 294920 | tf_op jit(solution)/shard_map/ppermute | solution.py:26
  3.7 2.6 %collective-permute-start.1 = (bf16[192,256]{1,0:T(8,128)(2,1)}, bf16[192,256]{1,0:T(8,128)(2,1)S(1)}, u32[]{:S(2)}, u32[]{:S(2)}) collective-permute-start(bf16[192,256]{1,0:T(8,128)(2,1)} %images_ref.1), channel_id=1, source_target_pairs={{0,2},{1,3},{2,0},{3,1},{4,6},{5,7},{6,4},{7,5},{8,10},{9,11},{10,... | collective-permute-start | bytes 294920 | tf_op jit(solution)/shard_map/ppermute | solution.py:26
  6.3 0.0 collective-permute-start.2
  6.3 0.4 collective-permute-done.refs_0_
  6.8 0.1 collective-permute-start.4
  6.9 0.9 %copy-done = bf16[192,256]{1,0:T(8,128)(2,1)S(1)} copy-done((bf16[192,256]{1,0:T(8,128)(2,1)S(1)}, bf16[192,256]{1,0:T(8,128)(2,1)}, u32[]{:S(2)}) %copy-start) | copy-done | bytes 98328
  7.8 1.8 %collective-permute-start.7 = (bf16[48,256]{1,0:T(8,128)(2,1)S(1)}, bf16[48,256]{1,0:T(8,128)(2,1)S(1)}, u32[]{:S(2)}, u32[]{:S(2)}) collective-permute-start(bf16[48,256]{1,0:T(8,128)(2,1)S(1)} %get-tuple-element.7), channel_id=1, source_target_pairs={{0,1},{1,0},{2,3},{3,2},{4,5},{5,4},{6,7},{7,6},{8,9},{9,8},{10,11... | collective-permute-start | bytes 73736 | tf_op jit(solution)/shard_map/ppermute | solution.py:26
  9.5 2.4 %collective-permute-done.7.refs_1_ = bf16[48,256]{1,0:T(8,128)(2,1)S(1)} collective-permute-done((bf16[48,256]{1,0:T(8,128)(2,1)S(1)}, bf16[48,256]{1,0:T(8,128)(2,1)S(1)}, u32[]{:S(2)}, u32[]{:S(2)}) %collective-permute-start.7) | collective-permute-done | bytes 24608 | tf_op jit(solution)/shard_map/ppermute | solution.py:26
  11.9 3.4 %collective-permute-start.8 = (bf16[48,256]{1,0:T(8,128)(2,1)S(1)}, bf16[48,256]{1,0:T(8,128)(2,1)S(1)}, u32[]{:S(2)}, u32[]{:S(2)}) collective-permute-start(bf16[48,256]{1,0:T(8,128)(2,1)S(1)} %get-tuple-element.8), channel_id=1, source_target_pairs={{0,2},{1,3},{2,0},{3,1},{4,6},{5,7},{6,4},{7,5},{8,10},{9,11},{10,... | collective-permute-start | bytes 73736 | tf_op jit(solution)/shard_map/ppermute | solution.py:26
  15.4 1.8 %collective-permute-done.8.refs_2_ = bf16[48,256]{1,0:T(8,128)(2,1)S(1)} collective-permute-done((bf16[48,256]{1,0:T(8,128)(2,1)S(1)}, bf16[48,256]{1,0:T(8,128)(2,1)S(1)}, u32[]{:S(2)}, u32[]{:S(2)}) %collective-permute-start.8) | collective-permute-done | bytes 24608 | tf_op jit(solution)/shard_map/ppermute | solution.py:26
  17.2 4.3 %collective-permute-start.9 = (bf16[48,256]{1,0:T(8,128)(2,1)S(1)}, bf16[48,256]{1,0:T(8,128)(2,1)S(1)}, u32[]{:S(2)}, u32[]{:S(2)}) collective-permute-start(bf16[48,256]{1,0:T(8,128)(2,1)S(1)} %get-tuple-element.9), channel_id=1, source_target_pairs={{0,3},{1,2},{2,1},{3,0},{4,7},{5,6},{6,5},{7,4},{8,11},{9,10},{10,... | collective-permute-start | bytes 73736 | tf_op jit(solution)/shard_map/ppermute | solution.py:26
  21.4 1.8 %collective-permute-done.9.refs_3_ = bf16[48,256]{1,0:T(8,128)(2,1)S(1)} collective-permute-done((bf16[48,256]{1,0:T(8,128)(2,1)S(1)}, bf16[48,256]{1,0:T(8,128)(2,1)S(1)}, u32[]{:S(2)}, u32[]{:S(2)}) %collective-permute-start.9) | collective-permute-done | bytes 24608 | tf_op jit(solution)/shard_map/ppermute | solution.py:26
  23.2 0.1 shard_map.54.refs_3_
  23.4 2.0 %collective-permute-start.10 = (bf16[48,1024]{1,0:T(8,128)(2,1)S(1)}, bf16[48,1024]{1,0:T(8,128)(2,1)S(1)}, u32[]{:S(2)}, u32[]{:S(2)}) collective-permute-start(bf16[48,1024]{1,0:T(8,128)(2,1)S(1)} %shard_map.54.refs_3_), channel_id=1, source_target_pairs={{0,8},{4,12},{8,0},{12,4},{16,24},{20,28},{24,16},{28,20},{1,9},{5... | collective-permute-start | bytes 294920 | tf_op jit(solution)/shard_map/ppermute | solution.py:26
  25.4 0.5 %collective-permute-start.6 = (bf16[192,256]{1,0:T(8,128)(2,1)S(1)}, bf16[192,256]{1,0:T(8,128)(2,1)S(1)}, u32[]{:S(2)}, u32[]{:S(2)}) collective-permute-start(bf16[192,256]{1,0:T(8,128)(2,1)S(1)} %collective-permute-done.2.refs_2_), channel_id=1, source_target_pairs={{0,4},{4,0},{8,12},{12,8},{16,20},{20,16},{24,28},{28,24},{1,5},{5... | collective-permute-start | bytes 294920 | tf_op jit(solution)/shard_map/ppermute | solution.py:26
  25.9 1.5 %collective-permute-start.11 = (bf16[48,1024]{1,0:T(8,128)(2,1)S(1)}, bf16[48,1024]{1,0:T(8,128)(2,1)S(1)}, u32[]{:S(2)}, u32[]{:S(2)}) collective-permute-start(bf16[48,1024]{1,0:T(8,128)(2,1)S(1)} %shard_map.54.refs_3_), channel_id=1, source_target_pairs={{0,16},{4,20},{8,24},{12,28},{16,0},{20,4},{24,8},{28,12},{1,17},{... | collective-permute-start | bytes 294920 | tf_op jit(solution)/shard_map/ppermute | solution.py:26
  27.4 0.0 collective-permute-start.12
  28.1 1.1 %shard_map.51.refs_1_ = bf16[192,1024]{1,0:T(8,128)(2,1)S(1)} custom-call(bf16[192,256]{1,0:T(8,128)(2,1)} %images_ref.1, bf16[192,256]{1,0:T(8,128)(2,1)S(1)} %collective-permute-done.refs_0_, bf16[192,256]{1,0:T(8,128)(2,1)S(1)} %collective-permute-done.1.refs_1_, bf16[192,256]{1,0:T(8,128)(2,1)S(1)} %collective-permute-done.2.refs_2_), custom_call_target="tpu_custom_call" | custom-call | tf_op jit(solution)/shard_map/pallas_call | solution.py:160
  29.3 0.2 shard_map.52.refs_2_
  29.5 2.3 %collective-permute-done.11.refs_5_ = bf16[48,1024]{1,0:T(8,128)(2,1)S(1)} collective-permute-done((bf16[48,1024]{1,0:T(8,128)(2,1)S(1)}, bf16[48,1024]{1,0:T(8,128)(2,1)S(1)}, u32[]{:S(2)}, u32[]{:S(2)}) %collective-permute-start.11) | collective-permute-done | bytes 98336 | tf_op jit(solution)/shard_map/ppermute | solution.py:26
  31.8 1.1 %collective-permute-done.12.refs_6_ = bf16[48,1024]{1,0:T(8,128)(2,1)S(1)} collective-permute-done((bf16[48,1024]{1,0:T(8,128)(2,1)S(1)}, bf16[48,1024]{1,0:T(8,128)(2,1)S(1)}, u32[]{:S(2)}, u32[]{:S(2)}) %collective-permute-start.12) | collective-permute-done | bytes 98336 | tf_op jit(solution)/shard_map/ppermute | solution.py:26
  32.9 0.6 %shard_map.55 = f32[32,4,128]{2,1,0:T(4,128)S(1)} custom-call(f32[1,1]{1,0:T(1,128)} %bitcast.1.scale_ref, f32[48,128]{1,0:T(8,128)S(1)} %shard_map.50.refs_0_, bf16[192,1024]{1,0:T(8,128)(2,1)S(1)} %shard_map.51.refs_1_, bf16[192,1024]{1,0:T(8,128)(2,1)S(1)} %shard_map.52.refs_2_, bf16[48,1024]{1,0:T(8,128)(2,1)S(1)} %shard_map.54.refs_3_, ...), custom_call_target="tpu_custom_call" | custom-call | tf_op jit(solution)/shard_map/pallas_call | solution.py:171
  33.5 11.8 %all_to_all.5.got_ref = f32[32,4,128]{2,1,0:T(4,128)S(1)} all-to-all(f32[32,4,128]{2,1,0:T(4,128)S(1)} %shard_map.55), channel_id=1, replica_groups=mesh['dp'=8,'mp'=4] {'dp','mp'}, dimensions={0} | all-to-all | bytes 131072 | tf_op jit(solution)/shard_map/all_to_all | solution.py:178
  45.4 0.7 %shard_map.56 = (f32[192]{0:T(256)}, f32[192]{0:T(256)}) custom-call(f32[32,4,128]{2,1,0:T(4,128)S(1)} %all_to_all.5.got_ref), custom_call_target="tpu_custom_call" | custom-call | tf_op jit(solution)/shard_map/pallas_call | solution.py:31
  (12 shorter events, 0.0 us)
Async XLA Ops:
  0.6 6.1 %collective-permute-start = (bf16[192,256]{1,0:T(8,128)(2,1)}, bf16[192,256]{1,0:T(8,128)(2,1)S(1)}, u32[]{:S(2)}, u32[]{:S(2)}) collective-permute-start(bf16[192,256]{1,0:T(8,128)(2,1)} %images_ref.1), channel_id=1, source_target_pairs={{0,1},{1,0},{2,3},{3,2},{4,5},{5,4},{6,7},{7,6},{8,9},{9,8},{10,11... | collective-permute-start | bytes 294920 | tf_op jit(solution)/shard_map/ppermute | solution.py:26
  3.7 21.6 %collective-permute-start.1 = (bf16[192,256]{1,0:T(8,128)(2,1)}, bf16[192,256]{1,0:T(8,128)(2,1)S(1)}, u32[]{:S(2)}, u32[]{:S(2)}) collective-permute-start(bf16[192,256]{1,0:T(8,128)(2,1)} %images_ref.1), channel_id=1, source_target_pairs={{0,2},{1,3},{2,0},{3,1},{4,6},{5,7},{6,4},{7,5},{8,10},{9,11},{10,... | collective-permute-start | bytes 294920 | tf_op jit(solution)/shard_map/ppermute | solution.py:26
  6.3 19.1 %collective-permute-start.2 = (bf16[192,256]{1,0:T(8,128)(2,1)}, bf16[192,256]{1,0:T(8,128)(2,1)S(1)}, u32[]{:S(2)}, u32[]{:S(2)}) collective-permute-start(bf16[192,256]{1,0:T(8,128)(2,1)} %images_ref.1), channel_id=1, source_target_pairs={{0,3},{1,2},{2,1},{3,0},{4,7},{5,6},{6,5},{7,4},{8,11},{9,10},{10,... | collective-permute-start | bytes 294920 | tf_op jit(solution)/shard_map/ppermute | solution.py:26
  6.3 19.6 %collective-permute-start.3 = (bf16[192,256]{1,0:T(8,128)(2,1)}, bf16[192,256]{1,0:T(8,128)(2,1)S(1)}, u32[]{:S(2)}, u32[]{:S(2)}) collective-permute-start(bf16[192,256]{1,0:T(8,128)(2,1)} %images_ref.1), channel_id=1, source_target_pairs={{0,4},{4,0},{8,12},{12,8},{16,20},{20,16},{24,28},{28,24},{1,5},{5... | collective-permute-start | bytes 294920 | tf_op jit(solution)/shard_map/ppermute | solution.py:26
  6.8 20.7 %collective-permute-start.4 = (bf16[192,256]{1,0:T(8,128)(2,1)S(1)}, bf16[192,256]{1,0:T(8,128)(2,1)S(1)}, u32[]{:S(2)}, u32[]{:S(2)}) collective-permute-start(bf16[192,256]{1,0:T(8,128)(2,1)S(1)} %collective-permute-done.refs_0_), channel_id=1, source_target_pairs={{0,4},{4,0},{8,12},{12,8},{16,20},{20,16},{24,28},{28,24},{1,5},{5... | collective-permute-start | bytes 294920 | tf_op jit(solution)/shard_map/ppermute | solution.py:26
  6.9 0.9 %copy-start = (bf16[192,256]{1,0:T(8,128)(2,1)S(1)}, bf16[192,256]{1,0:T(8,128)(2,1)}, u32[]{:S(2)}) copy-start(bf16[192,256]{1,0:T(8,128)(2,1)} %texts_ref.1) | copy-start | bytes 294916
  7.8 4.2 %collective-permute-start.7 = (bf16[48,256]{1,0:T(8,128)(2,1)S(1)}, bf16[48,256]{1,0:T(8,128)(2,1)S(1)}, u32[]{:S(2)}, u32[]{:S(2)}) collective-permute-start(bf16[48,256]{1,0:T(8,128)(2,1)S(1)} %get-tuple-element.7), channel_id=1, source_target_pairs={{0,1},{1,0},{2,3},{3,2},{4,5},{5,4},{6,7},{7,6},{8,9},{9,8},{10,11... | collective-permute-start | bytes 73736 | tf_op jit(solution)/shard_map/ppermute | solution.py:26
  11.9 5.2 %collective-permute-start.8 = (bf16[48,256]{1,0:T(8,128)(2,1)S(1)}, bf16[48,256]{1,0:T(8,128)(2,1)S(1)}, u32[]{:S(2)}, u32[]{:S(2)}) collective-permute-start(bf16[48,256]{1,0:T(8,128)(2,1)S(1)} %get-tuple-element.8), channel_id=1, source_target_pairs={{0,2},{1,3},{2,0},{3,1},{4,6},{5,7},{6,4},{7,5},{8,10},{9,11},{10,... | collective-permute-start | bytes 73736 | tf_op jit(solution)/shard_map/ppermute | solution.py:26
  17.2 6.1 %collective-permute-start.9 = (bf16[48,256]{1,0:T(8,128)(2,1)S(1)}, bf16[48,256]{1,0:T(8,128)(2,1)S(1)}, u32[]{:S(2)}, u32[]{:S(2)}) collective-permute-start(bf16[48,256]{1,0:T(8,128)(2,1)S(1)} %get-tuple-element.9), channel_id=1, source_target_pairs={{0,3},{1,2},{2,1},{3,0},{4,7},{5,6},{6,5},{7,4},{8,11},{9,10},{10,... | collective-permute-start | bytes 73736 | tf_op jit(solution)/shard_map/ppermute | solution.py:26
  23.4 6.1 %collective-permute-start.10 = (bf16[48,1024]{1,0:T(8,128)(2,1)S(1)}, bf16[48,1024]{1,0:T(8,128)(2,1)S(1)}, u32[]{:S(2)}, u32[]{:S(2)}) collective-permute-start(bf16[48,1024]{1,0:T(8,128)(2,1)S(1)} %shard_map.54.refs_3_), channel_id=1, source_target_pairs={{0,8},{4,12},{8,0},{12,4},{16,24},{20,28},{24,16},{28,20},{1,9},{5... | collective-permute-start | bytes 294920 | tf_op jit(solution)/shard_map/ppermute | solution.py:26
  25.4 3.9 %collective-permute-start.5 = (bf16[192,256]{1,0:T(8,128)(2,1)S(1)}, bf16[192,256]{1,0:T(8,128)(2,1)S(1)}, u32[]{:S(2)}, u32[]{:S(2)}) collective-permute-start(bf16[192,256]{1,0:T(8,128)(2,1)S(1)} %collective-permute-done.1.refs_1_), channel_id=1, source_target_pairs={{0,4},{4,0},{8,12},{12,8},{16,20},{20,16},{24,28},{28,24},{1,5},{5... | collective-permute-start | bytes 294920 | tf_op jit(solution)/shard_map/ppermute | solution.py:26
  25.4 3.9 %collective-permute-start.6 = (bf16[192,256]{1,0:T(8,128)(2,1)S(1)}, bf16[192,256]{1,0:T(8,128)(2,1)S(1)}, u32[]{:S(2)}, u32[]{:S(2)}) collective-permute-start(bf16[192,256]{1,0:T(8,128)(2,1)S(1)} %collective-permute-done.2.refs_2_), channel_id=1, source_target_pairs={{0,4},{4,0},{8,12},{12,8},{16,20},{20,16},{24,28},{28,24},{1,5},{5... | collective-permute-start | bytes 294920 | tf_op jit(solution)/shard_map/ppermute | solution.py:26
  25.9 5.9 %collective-permute-start.11 = (bf16[48,1024]{1,0:T(8,128)(2,1)S(1)}, bf16[48,1024]{1,0:T(8,128)(2,1)S(1)}, u32[]{:S(2)}, u32[]{:S(2)}) collective-permute-start(bf16[48,1024]{1,0:T(8,128)(2,1)S(1)} %shard_map.54.refs_3_), channel_id=1, source_target_pairs={{0,16},{4,20},{8,24},{12,28},{16,0},{20,4},{24,8},{28,12},{1,17},{... | collective-permute-start | bytes 294920 | tf_op jit(solution)/shard_map/ppermute | solution.py:26
  27.4 5.5 %collective-permute-start.12 = (bf16[48,1024]{1,0:T(8,128)(2,1)S(1)}, bf16[48,1024]{1,0:T(8,128)(2,1)S(1)}, u32[]{:S(2)}, u32[]{:S(2)}) collective-permute-start(bf16[48,1024]{1,0:T(8,128)(2,1)S(1)} %shard_map.54.refs_3_), channel_id=1, source_target_pairs={{0,24},{4,28},{8,16},{12,20},{16,8},{20,12},{24,0},{28,4},{1,25},{... | collective-permute-start | bytes 294920 | tf_op jit(solution)/shard_map/ppermute | solution.py:26
